TPU v7x, 32 devices: a whole 2x2x4 slice. The times are simulated.
32 devices in a mesh: seq: 4 (over y, core), fsdp: 8 (over z, x).
Axes of the slice: x: 2, y: 2, z: 4, core: 2. Of those that a mesh axis runs over, the one named last changes fastest.
Arguments:
- tokens: bfloat16 [8, 1536, 1024], P('fsdp', 'seq'), may hold values from -6 to 6
- lengths: int32 [8, 3], P('fsdp'), may hold values from 1 to 1024, 1536 in all within a row
- time_steps: int32 [8, 3], P('fsdp'), may hold values from 0 to 999
- order: int32 [8, 1536], P('fsdp', 'seq'), may hold values from 0 to 1535, each once within a row
- w_time: bfloat16 [256, 2048], P('fsdp'), may hold values from -0.375 to 0.375
- w_qkv: bfloat16 [1024, 3072], P('fsdp'), may hold values from -0.1875 to 0.1875
- w_out: bfloat16 [1024, 1024], P('fsdp'), may hold values from -1.5 to 1.5
- w_up: bfloat16 [1024, 4096], P('fsdp'), may hold values from -0.1875 to 0.1875
- w_down: bfloat16 [4096, 1024], P('fsdp'), may hold values from -0.09375 to 0.09375
- cotangent: bfloat16 [8, 1536, 1024], P('fsdp', 'seq'), may hold values from -6 to 6
Outputs:
- output: bfloat16 [8, 1536, 1024], P('fsdp', 'seq')
- input_grad: float32 [8, 1536, 1024], P('fsdp', 'seq')
- grad_time: float32 [256, 2048], P('fsdp')
- grad_qkv: float32 [1024, 3072], P('fsdp')
- grad_out: float32 [1024, 1024], P('fsdp')
- grad_up: float32 [1024, 4096], P('fsdp')
- grad_down: float32 [4096, 1024], P('fsdp')
Inputs may be any that keep to these rules, and one draw needn't show every extreme that they name: Each group's 3 lengths sum to 1536; the longest is exactly 1024. `order`: each group's row is a permutation of the indices 0 to 1535.
All inputs are finite; a program needn't handle non-finite values.
Results may differ from a plain program's by a relative error of at most 0.02.
Values may be sent and summed in bfloat16 or wider, within the bound.
A program may use at most 192 MiB of HBM per device.

v0:
```python
import math
import jax
import jax.numpy as jnp
from jax import lax
from jax.sharding import PartitionSpec as P

D = 1024
H = 16
HD = 64
TEMB = 256
NSEQ = 3
EPS = 1e-05
NEG = -1e30
BASE = 10000.0
BLOCK_ROWS = 512


def time_embedding(steps):
    half = TEMB // 2
    freqs = jnp.exp(-math.log(BASE) * jnp.arange(half, dtype=jnp.float32) / half)
    angles = steps.astype(jnp.float32)[:, None] * freqs[None, :]
    return jnp.concatenate([jnp.sin(angles), jnp.cos(angles)], axis=-1)


def layout(lens, places):
    ends = jnp.cumsum(lens)
    starts = ends - lens
    member = (places[:, None] >= starts[None, :]) & (places[:, None] < ends[None, :])
    labels = jnp.arange(NSEQ, dtype=jnp.int32)
    segment = jnp.sum(jnp.where(member, labels[None, :], 0), axis=1)
    offset = places - jnp.sum(jnp.where(member, starts[None, :], 0), axis=1)
    return (member.astype(jnp.float32), segment, offset)


def rotate(values, offset, sign):
    half = HD // 2
    freqs = jnp.exp(-math.log(BASE) * jnp.arange(half, dtype=jnp.float32) * 2.0 / HD)
    angles = offset.astype(jnp.float32)[:, None] * freqs[None, :]
    cosine = jnp.cos(angles)[:, None, :]
    sine = sign * jnp.sin(angles)[:, None, :]
    first = values[..., :half]
    second = values[..., half:]
    return jnp.concatenate(
        [first * cosine - second * sine, second * cosine + first * sine], axis=-1
    )


def norm_mod(values, scale):
    centre = jnp.mean(values, axis=-1, keepdims=True)
    centred = values - centre
    spread = jnp.mean(centred * centred, axis=-1, keepdims=True)
    return centred * lax.rsqrt(spread + EPS) * (1.0 + scale)


def contract_rows(left, right):
    return lax.dot_general(
        left, right, (((0,), (0,)), ((), ())), preferred_element_type=jnp.float32
    )


def contract_cols(left, right):
    return lax.dot_general(
        left, right, (((1,), (1,)), ((), ())), preferred_element_type=jnp.float32
    )


def weight_rows(left, weight):
    return (
        jnp.dot(
            left,
            lax.all_gather(weight, "fsdp", axis=0, tiled=True),
            preferred_element_type=jnp.float32,
        ),
        weight,
    )


def weight_cols(grad, weight):
    return contract_cols(grad, lax.all_gather(weight, "fsdp", axis=0, tiled=True))


def weight_grad(left, grad):

    def term():
        if grad.dtype == jnp.float32:
            return lax.dot_general(
                left.astype(jnp.float32),
                grad,
                (((0,), (0,)), ((), ())),
                precision=lax.Precision.HIGHEST,
                preferred_element_type=jnp.float32,
            )
        return contract_rows(left, grad)

    shard = lax.psum_scatter(
        term().astype(jnp.bfloat16), "fsdp", scatter_dimension=0, tiled=True
    ).astype(jnp.float32)
    shard = lax.psum(shard.astype(jnp.bfloat16), "seq").astype(jnp.float32)
    return shard


def to_heads(packed):
    return lax.all_to_all(packed, "seq", split_axis=2, concat_axis=0, tiled=True)


def to_rows(packed):
    return lax.all_to_all(packed, "seq", split_axis=0, concat_axis=2, tiled=True)


def reorder(data, wanted, labels):
    pick = (wanted[:, None] == labels[None, :]).astype(jnp.bfloat16)
    return jnp.dot(
        pick, lax.all_gather(data, "seq", axis=0, tiled=True), preferred_element_type=jnp.float32
    )


def slice_cols(matrix, start):
    return lax.dynamic_slice_in_dim(matrix, start, HD, 1)


def head_forward(query, key, value, segment, block):
    group = query.shape[0]
    factor = HD ** (-0.5)

    def one_block(index):
        start = index * block
        q_blk = lax.dynamic_slice_in_dim(query, start, block, 0)
        s_blk = lax.dynamic_slice_in_dim(segment, start, block, 0)
        scores = contract_cols(q_blk, key) * factor
        scores = jnp.where(s_blk[:, None] == segment[None, :], scores, NEG)
        peak = jnp.max(scores, axis=1, keepdims=True)
        expo = jnp.exp(scores - peak)
        total = jnp.sum(expo, axis=1, keepdims=True)
        probs = (expo / total).astype(jnp.bfloat16)
        mixed = jnp.dot(probs, value, preferred_element_type=jnp.float32)
        return (mixed.astype(jnp.bfloat16), (peak + jnp.log(total))[:, 0])

    mixed, logsum = lax.map(one_block, jnp.arange(group // block))
    return (mixed.reshape(group, HD), logsum.reshape(group))


def head_backward(query, key, value, logsum, d_mixed, segment, offset, block):
    group = query.shape[0]
    factor = HD ** (-0.5)

    def step(carry, index):
        d_key, d_value = carry
        start = index * block
        q_blk = lax.dynamic_slice_in_dim(query, start, block, 0)
        s_blk = lax.dynamic_slice_in_dim(segment, start, block, 0)
        l_blk = lax.dynamic_slice_in_dim(logsum, start, block, 0)
        g_blk = lax.dynamic_slice_in_dim(d_mixed, start, block, 0)
        scores = contract_cols(q_blk, key) * factor
        probs = jnp.where(s_blk[:, None] == segment[None, :], jnp.exp(scores - l_blk[:, None]), 0.0)
        probs_low = probs.astype(jnp.bfloat16)
        d_value = d_value + contract_rows(probs_low, g_blk)
        d_probs = contract_cols(g_blk, value)
        delta = jnp.sum(probs * d_probs, axis=1, keepdims=True)
        d_scores = (probs * (d_probs - delta)).astype(jnp.bfloat16)
        d_query = jnp.dot(d_scores, key, preferred_element_type=jnp.float32) * factor
        d_key = d_key + contract_rows(d_scores, q_blk) * factor
        return ((d_key, d_value), d_query)

    zeros = jnp.zeros((group, HD), jnp.float32)
    (d_key, d_value), d_query = lax.scan(step, (zeros, zeros), jnp.arange(group // block))
    d_query = d_query.reshape(group, HD)
    back_query = rotate(d_query[:, None, :], offset, -1.0)[:, 0, :]
    back_key = rotate(d_key[:, None, :], offset, -1.0)[:, 0, :]
    return (back_query, back_key, d_value)


def on_device(tokens, lengths, time_steps, order, w_time, w_qkv, w_out, w_up, w_down, cotangent):
    rows = tokens.shape[1]
    slices = lax.axis_size("seq")
    local_heads = H // slices
    group = rows * slices
    block = min(BLOCK_ROWS, group)
    lens = lengths[0]
    places = order[0]
    order_all = lax.all_gather(places, "seq", axis=0, tiled=True)
    member_mine, segment_mine, offset_mine = layout(lens, places)
    member_all, segment_all, offset_all = layout(lens, order_all)
    emb = time_embedding(time_steps[0]).astype(jnp.bfloat16)
    scales_seq, whole_time = weight_rows(emb, w_time)
    scales = jnp.dot(member_mine, scales_seq, precision=lax.Precision.HIGHEST)
    scale_one = scales[:, :D]
    scale_two = scales[:, D:]
    inputs = tokens[0].astype(jnp.float32)
    normed_one, pull_one = jax.vjp(norm_mod, inputs, scale_one)
    h_one = normed_one.astype(jnp.bfloat16)
    projected, whole_qkv = weight_rows(h_one, w_qkv)
    query = rotate(projected[:, :D].reshape(rows, H, HD), offset_mine, 1.0).reshape(rows, D)
    key = rotate(projected[:, D : 2 * D].reshape(rows, H, HD), offset_mine, 1.0).reshape(rows, D)
    packed = jnp.stack([query, key, projected[:, 2 * D :]], axis=1).astype(jnp.bfloat16)
    heads_qkv = to_heads(packed.reshape(rows, 3, slices, local_heads * HD))
    q_heads = heads_qkv[:, 0, 0]
    k_heads = heads_qkv[:, 1, 0]
    v_heads = heads_qkv[:, 2, 0]

    def forward_head(index):
        start = index * HD
        return head_forward(
            slice_cols(q_heads, start),
            slice_cols(k_heads, start),
            slice_cols(v_heads, start),
            segment_all,
            block,
        )

    mixed_heads, logsum_heads = lax.map(forward_head, jnp.arange(local_heads))
    mixed_cat = mixed_heads.transpose(1, 0, 2).reshape(group, 1, 1, local_heads * HD)
    mixed = to_rows(mixed_cat).reshape(rows, D)
    attn_out, whole_out = weight_rows(mixed, w_out)
    x_two = inputs + attn_out
    normed_two, pull_two = jax.vjp(norm_mod, x_two, scale_two)
    h_two = normed_two.astype(jnp.bfloat16)
    up, whole_up = weight_rows(h_two, w_up)
    activated, pull_gelu = jax.vjp(jax.nn.gelu, up)
    hidden = activated.astype(jnp.bfloat16)
    ffn_out, whole_down = weight_rows(hidden, w_down)
    result = (x_two + ffn_out).astype(jnp.bfloat16)
    mine = lax.axis_index("seq") * rows + jnp.arange(rows, dtype=jnp.int32)
    output = reorder(result, mine, order_all).astype(jnp.bfloat16)
    every = jnp.arange(group, dtype=jnp.int32)
    d_result = reorder(cotangent[0], places, every)
    d_low = d_result.astype(jnp.bfloat16)
    d_hidden = weight_cols(d_low, w_down)
    grad_down = weight_grad(hidden, d_low)
    d_up = pull_gelu(d_hidden)[0].astype(jnp.bfloat16)
    grad_up = weight_grad(h_two, d_up)
    d_htwo = weight_cols(d_up, w_up)
    d_xpart, d_scale_two = pull_two(d_htwo)
    d_xtwo = d_result + d_xpart
    d_attn = d_xtwo.astype(jnp.bfloat16)
    grad_out = weight_grad(mixed, d_attn)
    d_mixed = weight_cols(d_attn, w_out).astype(jnp.bfloat16)
    d_heads = to_heads(d_mixed.reshape(rows, 1, slices, local_heads * HD))[:, 0, 0]

    def backward_head(index):
        start = index * HD
        return head_backward(
            slice_cols(q_heads, start),
            slice_cols(k_heads, start),
            slice_cols(v_heads, start),
            logsum_heads[index],
            slice_cols(d_heads, start),
            segment_all,
            offset_all,
            block,
        )

    d_query, d_key, d_value = lax.map(backward_head, jnp.arange(local_heads))
    stacked = jnp.stack([d_query, d_key, d_value], axis=1)
    stacked = (
        stacked.transpose(2, 1, 0, 3).reshape(group, 3, 1, local_heads * HD).astype(jnp.bfloat16)
    )
    d_qkv = to_rows(stacked).reshape(rows, 3 * D)
    grad_qkv = weight_grad(h_one, d_qkv)
    d_hone = weight_cols(d_qkv, w_qkv)
    d_xone, d_scale_one = pull_one(d_hone)
    input_grad = d_xtwo + d_xone
    d_scales = lax.dot_general(
        member_mine,
        jnp.concatenate([d_scale_one, d_scale_two], axis=1),
        (((0,), (0,)), ((), ())),
        precision=lax.Precision.HIGHEST,
        preferred_element_type=jnp.float32,
    )
    grad_time = weight_grad(emb, d_scales)
    grads = (grad_time, grad_qkv, grad_out, grad_up, grad_down)
    return (output[None], input_grad[None], grads[0], grads[1], grads[2], grads[3], grads[4])


def solution(mesh):
    return jax.shard_map(
        on_device,
        mesh=mesh,
        in_specs=(
            P("fsdp", "seq", None),
            P("fsdp", None),
            P("fsdp", None),
            P("fsdp", "seq"),
            P("fsdp", None),
            P("fsdp", None),
            P("fsdp", None),
            P("fsdp", None),
            P("fsdp", None),
            P("fsdp", "seq", None),
        ),
        out_specs=(
            P("fsdp", "seq", None),
            P("fsdp", "seq", None),
            P("fsdp", None),
            P("fsdp", None),
            P("fsdp", None),
            P("fsdp", None),
            P("fsdp", None),
        ),
        check_vma=False,
    )
```

profile of v0, /device:TPU:0, one launch (start us, length us, event | category | flops | bytes accessed | tf_op | source)
XLA Modules:
  0.0 1447.6 jit_solution(13211309296788337764)
XLA Ops:
  11.9 41.2 %all-gather.10.cloned.1.call-done = bf16[256,2048]{1,0:T(8,128)(2,1)} async-done(((bf16[32,2048]{1,0:T(8,128)(2,1)}), bf16[256,2048]{1,0:T(8,128)(2,1)}) %all-gather.10.cloned.1.call-update) | async-done | bytes 1048592 | tf_op jit(solution)/shard_map/all_gather | solution.py:71
  58.2 94.6 %all-gather.12.cloned.1.call-done = bf16[1024,3072]{1,0:T(8,128)(2,1)} async-done(((bf16[128,3072]{1,0:T(8,128)(2,1)}), bf16[1024,3072]{1,0:T(8,128)(2,1)}) %all-gather.12.cloned.1.call-update) | async-done | bytes 6291472 | tf_op jit(solution)/shard_map/all_gather | solution.py:71
  152.8 4.7 fusion.97
  174.5 31.2 %all-gather = s32[1,1536]{1,0:T(1,128)S(1)} all-gather(s32[1,384]{1,0:T(1,128)S(1)} %copy-done.57), channel_id=2, replica_groups=mesh['seq'=4,'fsdp'=8] {'seq'}, dimensions={1}, use_global_device_ids=true | all-gather | bytes 7680 | tf_op jit(solution)/shard_map/all_gather | solution.py:180
  212.0 64.9 %while.88 = (s32[]{:T(128)}, bf16[4,1536,64]{1,2,0:T(8,128)(2,1)S(1)}, f32[4,1536]{1,0:T(4,128)}, s32[4]{0:T(128)S(1)}, bf16[1536,256]{1,0:T(8,128)(2,1)}, /*ind...) while((s32[]{:T(128)}, ...), condition=%wide.region_10.11_spmd, body=%wide.region_5.0_spmd.sunk | while | flops 208436736 | bytes 12839458 | solution.py:210
  215.7 10.6 while.91
  231.9 10.6 while.91
  248.2 10.6 while.91
  264.4 10.6 while.91
  279.9 3.7 all-to-all-start.1
  283.6 4.5 fusion.49
  288.1 7.1 all-to-all-done.1
  302.8 59.8 %all-gather.16.cloned.1.call-done = bf16[1024,4096]{1,0:T(8,128)(2,1)} async-done(((bf16[128,4096]{1,0:T(8,128)(2,1)}), bf16[1024,4096]{1,0:T(8,128)(2,1)}) %all-gather.16.cloned.1.call-update) | async-done | bytes 8388624 | tf_op jit(solution)/shard_map/all_gather | solution.py:71
  362.6 9.9 fusion.98
  372.5 114.8 %all-gather.18.cloned.1.call-done = bf16[4096,1024]{1,0:T(8,128)(2,1)} async-done(((bf16[512,1024]{1,0:T(8,128)(2,1)}), bf16[4096,1024]{1,0:T(8,128)(2,1)}) %all-gather.18.cloned.1.call-update) | async-done | bytes 8388624 | tf_op jit(solution)/shard_map/all_gather | solution.py:71
  487.2 10.7 fusion.44
  498.0 3.8 multiply_reduce_fusion.1
  517.0 8.2 all-to-all-done.2
  525.7 255.7 %while.90 = (s32[]{:T(128)}, bf16[4,1536,64]{1,2,0:T(8,128)(2,1)}, bf16[4,1536,64]{1,2,0:T(8,128)(2,1)}, bf16[4,1536,64]{1,2,0:T(8,128)(2,1)}, s32[4]{0:T(128)},...) while((s32[]{:T(128)}, bf16[4,1536,64]{1,2,0:T(8,128)(2,1)}, ...), condition=%wide.region_20.21_spmd, body=%wide.region_16.20_spmd.sunk | while | flops 513375776 | bytes 57267424 | solution.py:252
  535.7 48.1 %while.92 = (s32[]{:T(128)}, f32[1536,64]{0,1:T(8,128)}, f32[1536,64]{0,1:T(8,128)}, f32[3,512,64]{1,0,2:T(4,128)}, s32[3]{0:T(128)}, /*index=5*/s32[1536]{0:T(1...) while((s32[]{:T(128)}, f32[1536,64]{0,1:T(8,128)}, ...), condition=%wide.region_19.19_spmd.clone, body=%wide.region_17.18_spmd.clone.sunk | while | flops 511704576 | bytes 37968256 | solution.py:165
  548.1 3.7 dynamic_update_slice.65
  564.2 3.6 dynamic_update_slice.65
  580.2 3.6 dynamic_update_slice.65
  599.7 48.1 %while.92 = (s32[]{:T(128)}, f32[1536,64]{0,1:T(8,128)}, f32[1536,64]{0,1:T(8,128)}, f32[3,512,64]{1,0,2:T(4,128)}, s32[3]{0:T(128)}, /*index=5*/s32[1536]{0:T(1...) while((s32[]{:T(128)}, f32[1536,64]{0,1:T(8,128)}, ...), condition=%wide.region_19.19_spmd.clone, body=%wide.region_17.18_spmd.clone.sunk | while | flops 511704576 | bytes 37968256 | solution.py:165
  612.0 3.6 dynamic_update_slice.65
  628.1 3.6 dynamic_update_slice.65
  644.1 3.6 dynamic_update_slice.65
  663.6 48.1 %while.92 = (s32[]{:T(128)}, f32[1536,64]{0,1:T(8,128)}, f32[1536,64]{0,1:T(8,128)}, f32[3,512,64]{1,0,2:T(4,128)}, s32[3]{0:T(128)}, /*index=5*/s32[1536]{0:T(1...) while((s32[]{:T(128)}, f32[1536,64]{0,1:T(8,128)}, ...), condition=%wide.region_19.19_spmd.clone, body=%wide.region_17.18_spmd.clone.sunk | while | flops 511704576 | bytes 37968256 | solution.py:165
  675.9 3.6 dynamic_update_slice.65
  692.0 3.6 dynamic_update_slice.65
  708.1 3.6 dynamic_update_slice.65
  727.5 48.1 %while.92 = (s32[]{:T(128)}, f32[1536,64]{0,1:T(8,128)}, f32[1536,64]{0,1:T(8,128)}, f32[3,512,64]{1,0,2:T(4,128)}, s32[3]{0:T(128)}, /*index=5*/s32[1536]{0:T(1...) while((s32[]{:T(128)}, f32[1536,64]{0,1:T(8,128)}, ...), condition=%wide.region_19.19_spmd.clone, body=%wide.region_17.18_spmd.clone.sunk | while | flops 511704576 | bytes 37968256 | solution.py:165
  739.8 3.6 dynamic_update_slice.65
  784.7 4.3 copy.79
  789.0 39.8 %all_to_all.63 = bf16[1536,3,1,256]{3,1,2,0:T(4,128)(2,1)S(1)} all-to-all(bf16[1536,3,1,256]{3,1,2,0:T(4,128)(2,1)S(1)} %copy.79), channel_id=1, replica_groups=mesh['seq'=4,'fsdp'=8] {'seq'}, dimensions={0} | all-to-all | bytes 4718592 | tf_op jit(solution)/shard_map/all_to_all | solution.py:107
  830.5 4.5 copy.81
  835.0 6.7 fusion.63
  846.9 5.6 convolution_convert_fusion.2
  853.6 8.6 convolution_convert_fusion.1
  863.6 10.8 convolution_convert_fusion
  875.8 10.1 add_convert_fusion
  886.0 22.6 %reduce-scatter.6.cloned.1.call-done = bf16[32,2048]{1,0:T(8,128)(2,1)} async-done(((bf16[256,2048]{1,0:T(8,128)(2,1)}), bf16[32,2048]{1,0:T(8,128)(2,1)}) %reduce-scatter.6.cloned.1.call-update) | async-done | bytes 131088 | tf_op jit(solution)/shard_map/reduce_scatter | solution.py:95
  908.6 120.7 %reduce-scatter.8.cloned.1.call-done = bf16[128,3072]{1,0:T(8,128)(2,1)} async-done(((bf16[1024,3072]{1,0:T(8,128)(2,1)}), bf16[128,3072]{1,0:T(8,128)(2,1)}) %reduce-scatter.8.cloned.1.call-update) | async-done | bytes 786448 | tf_op jit(solution)/shard_map/reduce_scatter | solution.py:95
  1029.3 150.2 %reduce-scatter.12.cloned.1.call-done = bf16[128,4096]{1,0:T(8,128)(2,1)} async-done(((bf16[1024,4096]{1,0:T(8,128)(2,1)}), bf16[128,4096]{1,0:T(8,128)(2,1)}) %reduce-scatter.12.cloned.1.call-update) | async-done | bytes 1048592 | tf_op jit(solution)/shard_map/reduce_scatter | solution.py:95
  1179.5 150.2 %reduce-scatter.14.cloned.1.call-done = bf16[512,1024]{1,0:T(8,128)(2,1)} async-done(((bf16[4096,1024]{1,0:T(8,128)(2,1)}), bf16[512,1024]{1,0:T(8,128)(2,1)}) %reduce-scatter.14.cloned.1.call-update) | async-done | bytes 1048592 | tf_op jit(solution)/shard_map/reduce_scatter | solution.py:95
  1331.2 28.2 %all-gather.20.cloned.1.call-done = bf16[1536,1024]{1,0:T(8,128)(2,1)} async-done(((bf16[384,1024]{1,0:T(8,128)(2,1)}), bf16[1536,1024]{1,0:T(8,128)(2,1)}) %all-gather.20.cloned.1.call-update) | async-done | bytes 3145744 | tf_op jit(solution)/shard_map/all_gather | solution.py:113
  1359.4 4.2 fusion.69
  1363.6 69.2 %all-reduce.3.cloned.1.call-done = (bf16[32,2048]{1,0:T(8,128)(2,1)}, bf16[128,3072]{1,0:T(8,128)(2,1)}, bf16[128,1024]{1,0:T(8,128)(2,1)}, bf16[128,4096]{1,0:T(8,128)(2,1)}, bf16[512,1024]{1,0:T(8,128)(2,1)}) async-done(((bf16[32,2048]{1,0:T(8,128)(2,1)}, bf16[128,3072]{1,0:T(8,128)(2,1)}, bf16[128,1024]{1,0:T(8,128)(2,1)}, bf16[128,4096]{1,0:T(8,128)(2,1)}, bf16[512,1024]{1,0:T(8,128)(2,1)}), ...) | async-done | bytes 3276816 | tf_op jit(solution)/shard_map/psum | solution.py:98
  (683 shorter events, 338.7 us)
Async XLA Ops:
  7.2 46.0 %all-gather.10.cloned.1.call-start = ((), (), s32[]{:S(2)}) async-start(), calls=%async_computation.9 | async-start | bytes 1179648 | tf_op jit(solution)/shard_map/all_gather | solution.py:71
  7.9 144.8 %all-gather.12.cloned.1.call-start = ((), (), s32[]{:S(2)}) async-start(), calls=%async_computation.10 | async-start | bytes 7077888 | tf_op jit(solution)/shard_map/all_gather | solution.py:71
  8.7 274.9 %all-gather.22.cloned.1.call-start = ((), (), s32[]{:S(2)}) async-start(), calls=%async_computation.20 | async-start | bytes 3932160 | tf_op jit(solution)/shard_map/all_gather | solution.py:113
  9.4 287.7 %all-gather.14.cloned.1.call-start = ((), (), s32[]{:S(2)}) async-start(), calls=%async_computation.11 | async-start | bytes 2359296 | tf_op jit(solution)/shard_map/all_gather | solution.py:71
  10.0 352.6 %all-gather.16.cloned.1.call-start = ((), (), s32[]{:S(2)}) async-start(), calls=%async_computation.12 | async-start | bytes 9437184 | tf_op jit(solution)/shard_map/all_gather | solution.py:71
  10.6 44.0 %copy-start.39 = (s32[384]{0:T(512)}, s32[384]{0:T(512)S(1)}, u32[]{:S(2)}) copy-start(s32[384]{0:T(512)S(1)} %reduce.4) | copy-start | bytes 4612
  10.8 195.0 %copy-start.53 = (s32[3,1]{0,1:T(1,128)}, s32[3,1]{0,1:T(1,128)S(1)}, u32[]{:S(2)}) copy-start(s32[3,1]{0,1:T(1,128)S(1)} %reduce-window.4) | copy-start | bytes 40
  10.9 194.9 %copy-start.55 = (s32[3]{0:T(128)}, s32[3]{0:T(128)S(1)}, u32[]{:S(2)}) copy-start(s32[3]{0:T(128)S(1)} %fusion.87) | copy-start | bytes 40
  11.1 45.0 %copy-start.43 = (f32[384]{0:T(512)}, f32[384]{0:T(512)S(1)}, u32[]{:S(2)}) copy-start(f32[384]{0:T(512)S(1)} %broadcast_multiply_fusion.1) | copy-start | bytes 4612
  11.5 41.7 %copy-start.45 = (f32[384]{0:T(512)}, f32[384]{0:T(512)S(1)}, u32[]{:S(2)}) copy-start(f32[384]{0:T(512)S(1)} %fusion.62) | copy-start | bytes 4612
  11.6 43.0 %copy-start.49 = (bf16[3,128]{1,0:T(4,128)(2,1)}, bf16[3,128]{1,0:T(4,128)(2,1)S(1)}, u32[]{:S(2)}) copy-start(bf16[3,128]{1,0:T(4,128)(2,1)S(1)} %get-tuple-element.551) | copy-start | bytes 2308
  11.6 43.0 %copy-start.51 = (bf16[3,128]{1,0:T(4,128)(2,1)}, bf16[3,128]{1,0:T(4,128)(2,1)S(1)}, u32[]{:S(2)}) copy-start(bf16[3,128]{1,0:T(4,128)(2,1)S(1)} %get-tuple-element.552) | copy-start | bytes 2308
  11.7 46.5 %copy-start.47 = (f32[384]{0:T(512)}, f32[384]{0:T(512)S(1)}, u32[]{:S(2)}) copy-start(f32[384]{0:T(512)S(1)} %fusion.84) | copy-start | bytes 4612
  58.2 99.3 %copy-start.32 = (bf16[384,1024]{1,0:T(8,128)(2,1)}, bf16[384,1024]{1,0:T(8,128)(2,1)S(1)}, u32[]{:S(2)}) copy-start(bf16[384,1024]{1,0:T(8,128)(2,1)S(1)} %fusion.61) | copy-start | bytes 2359300
  170.3 36.2 %all-to-all-start = ((bf16[384,3,4,256]{0,3,1,2:T(8,128)(2,1)}), bf16[384,3,4,256]{0,3,1,2:T(8,128)(2,1)S(1)}, u32[]{:S(2)}, u32[]{:S(2)}) async-start(bf16[384,3,4,256]{0,3,1,2:T(8,128)(2,1)} %copy.73), calls=%async_computation | async-start | bytes 4718592 | tf_op jit(solution)/shard_map/all_to_all | solution.py:103
  173.9 313.3 %all-gather.18.cloned.1.call-start = ((), (), s32[]{:S(2)}) async-start(), calls=%async_computation.13 | async-start | bytes 9437184 | tf_op jit(solution)/shard_map/all_gather | solution.py:71
  278.6 5.0 copy-start.40
  279.9 15.2 %all-to-all-start.1 = ((bf16[4,2,49152]{2,1,0:T(2,128)(2,1)}), bf16[4,2,49152]{2,1,0:T(2,128)(2,1)S(1)}, u32[]{:S(2)}, u32[]{:S(2)}) async-start(bf16[4,2,49152]{2,1,0:T(2,128)(2,1)} %reshape.383), calls=%async_computation.1 | async-start | bytes 1572864 | tf_op jit(solution)/shard_map/all_to_all | solution.py:107
  487.2 10.8 copy-start.11
  487.2 10.8 copy-start.58
  505.2 9.1 copy-start.15
  507.1 6.6 copy-start.37
  507.1 6.6 copy-start.42
  507.1 7.2 copy-start.19
  510.1 15.1 %all-to-all-start.2 = ((bf16[384,1,4,256]{3,0,1,2:T(8,128)(2,1)}), bf16[384,1,4,256]{3,0,1,2:T(8,128)(2,1)S(1)}, u32[]{:S(2)}, u32[]{:S(2)}) async-start(bf16[384,1,4,256]{3,0,1,2:T(8,128)(2,1)} %copy.78), calls=%async_computation.2 | async-start | bytes 1572864 | tf_op jit(solution)/shard_map/all_to_all | solution.py:103
  513.6 372.4 %reduce-scatter.10.cloned.1.call-start = ((), (), s32[]{:S(2)}) async-start(), calls=%async_computation.17 | async-start | bytes 2359296 | tf_op jit(solution)/shard_map/reduce_scatter | solution.py:95
  516.9 391.7 %reduce-scatter.6.cloned.1.call-start = ((), (), s32[]{:S(2)}) async-start(), calls=%async_computation.15 | async-start | bytes 1179648 | tf_op jit(solution)/shard_map/reduce_scatter | solution.py:95
  525.7 10.0 copy-start.17
  583.9 4.9 copy-start.30
  583.9 5.8 copy-start.18
  589.7 10.0 copy-start.17
  647.8 5.8 copy-start.18
  653.6 10.0 copy-start.17
  711.7 5.8 copy-start.18
  717.5 10.0 copy-start.17
  775.6 5.8 copy-start.18
  835.0 6.7 copy-start.46
  835.0 6.7 copy-start.14
  835.0 6.7 copy-start.48
  846.8 182.5 %reduce-scatter.8.cloned.1.call-start = ((), (), s32[]{:S(2)}) async-start(), calls=%async_computation.16 | async-start | bytes 7077888 | tf_op jit(solution)/shard_map/reduce_scatter | solution.py:95
  852.5 327.0 %reduce-scatter.12.cloned.1.call-start = ((), (), s32[]{:S(2)}) async-start(), calls=%async_computation.18 | async-start | bytes 9437184 | tf_op jit(solution)/shard_map/reduce_scatter | solution.py:95
  862.2 467.5 %reduce-scatter.14.cloned.1.call-start = ((), (), s32[]{:S(2)}) async-start(), calls=%async_computation.19 | async-start | bytes 9437184 | tf_op jit(solution)/shard_map/reduce_scatter | solution.py:95
  874.4 485.0 %all-gather.20.cloned.1.call-start = ((), (), s32[]{:S(2)}) async-start(), calls=%async_computation.14 | async-start | bytes 3932160 | tf_op jit(solution)/shard_map/all_gather | solution.py:113
  885.9 443.9 %copy-start.16 = (f32[384,1024]{1,0:T(8,128)S(1)}, f32[384,1024]{1,0:T(8,128)}, u32[]{:S(2)}) copy-start(f32[384,1024]{1,0:T(8,128)} %copy-done.15) | copy-start | bytes 4718596
  885.9 443.9 %copy-start.21 = (f32[384,1024]{1,0:T(8,128)S(1)}, f32[384,1024]{1,0:T(8,128)}, u32[]{:S(2)}) copy-start(f32[384,1024]{1,0:T(8,128)} %get-tuple-element.519) | copy-start | bytes 4718596
  885.9 546.9 %all-reduce.3.cloned.1.call-start = ((), (), s32[]{:S(2)}) async-start(), calls=%async_computation.21 | async-start | bytes 6553600 | tf_op jit(solution)/shard_map/psum | solution.py:98
  1329.8 29.6 %copy-start.38 = (s32[1536]{0:T(1024)S(1)}, s32[1536]{0:T(1024)}, u32[]{:S(2)}) copy-start(s32[1536]{0:T(1024)} %copy-done.36) | copy-start | bytes 18436
  1432.8 5.0 copy-start.29
  (100 other events, 266.5 us)
Sparse Core Ops, SparseCore 0:
  10.1 42.9 all-gather.9
  55.4 97.3 all-gather.11
  154.4 29.1 all-gather.21
  185.5 51.9 all-gather.13
  239.5 123.0 all-gather.15
  364.5 122.6 all-gather.17
  518.5 67.2 reduce-scatter.9
  847.0 61.6 reduce-scatter.5
  912.2 117.0 reduce-scatter.7
  1032.8 146.6 reduce-scatter.11
  1183.1 146.5 reduce-scatter.13
  1331.7 27.6 all-gather.19
  1362.1 70.6 all-reduce.2
where the time goes:
time: 1460 us; the launch traced here: 1450 us
  waiting for transfers between devices  871 us (60%)
  matrix products  213 us (15%)
  local copies, waits for them, and re-layouts  174 us (12%)
  blocking collectives  71 us (5%)
  other arithmetic  65.3 us (4%)
  loops' own time  27.9 us (2%)
  between operations  14.8 us (1%)
    reduce_scatter x5, waiting for transfers between devices, weight_grad(): lax.psum_scatter(term().astype(jnp.bfloat16), 'fsdp', scatter_dimension=0...  444 us
    all_gather x5, waiting for transfers between devices, weight_rows(): lax.all_gather(weight, 'fsdp', axis=0, tiled=True)  310 us
    dot_general x28, matrix products, contract_rows(): lax.dot_general(left, right, (((0,), (0,)), ((), ())), preferred_element_...  78.2 us
    dot_general x40, matrix products, contract_cols(): lax.dot_general(left, right, (((1,), (1,)), ((), ())), preferred_element_...  74.3 us
    psum x1, waiting for transfers between devices, weight_grad(): shard = lax.psum(shard.astype(jnp.bfloat16), 'seq').astype(jnp.float32)  69.2 us
    dynamic_update_slice x24, local copies, waits for them, and re-layouts, head_backward(): lax.scan(step, (zeros, zeros), jnp.arange(group // block))  45.4 us
    all_to_all x1, blocking collectives, to_rows(): lax.all_to_all(packed, 'seq', split_axis=0, concat_axis=2, tiled=True)  39.8 us
    all_gather x1, blocking collectives, on_device(): order_all = lax.all_gather(places, 'seq', axis=0, tiled=True)  31.2 us
  transfers between devices with their start and end apart: 16, of which 12 were waited for; matrix products, arithmetic and copies ran while one was open for 28% of the time, Pallas kernels for 0%

commit v1 on v0

--- a/solution.py
+++ b/solution.py
@@ -13,6 +13,24 @@
 NEG = -1e30
 BASE = 10000.0
 BLOCK_ROWS = 512
+
+
+def remake_matrix(array_here, pos_dim):
+    array_here = jnp.moveaxis(array_here, 0, pos_dim)
+    new = array_here.shape
+    return array_here.reshape(*new[:pos_dim], new[pos_dim] * new[pos_dim + 1], *new[pos_dim + 2 :])
+
+
+def _place_samples(row_data, net_axis):
+    main = lax.psum(1, net_axis)
+    block_now, val = (main, lax.axis_index(net_axis))
+    big, reached = (row_data[None], 1)
+    while reached < block_now:
+        t1 = lax.ppermute(big, net_axis, [(dd, dd ^ reached) for dd in range(block_now)])
+        u_next = val & reached == 0
+        big = jnp.concatenate([jnp.where(u_next, big, t1), jnp.where(u_next, t1, big)])
+        reached *= 2
+    return big
 
 
 def time_embedding(steps):
@@ -65,12 +83,12 @@
 
 
 def weight_rows(left, weight):
+
+    def answer_knots(load, patch, axis_k):
+        return remake_matrix(_place_samples(load, patch), axis_k)
+
     return (
-        jnp.dot(
-            left,
-            lax.all_gather(weight, "fsdp", axis=0, tiled=True),
-            preferred_element_type=jnp.float32,
-        ),
+        jnp.dot(left, answer_knots(weight, "fsdp", 0), preferred_element_type=jnp.float32),
         weight,
     )
 

time: 1460 us -> 2000 us (1.37)
  waiting for transfers between devices: 871 us -> 1270 us
  local copies, waits for them, and re-layouts: 174 us -> 246 us
  other arithmetic: 65.3 us -> 103 us
  matrix products: 213 us -> 248 us
  blocking collectives: 71 us -> 44.8 us
    ppermute x0 -> x15, waiting for transfers between devices: none -> 948 us  [_place_samples(): lax.ppermute(big, net_axis, [(dd, dd ^ reached) for dd in range(block_now)])]
    all_gather x5 -> x4, waiting for transfers between devices: 310 us -> 0.04 us  [weight_cols(): lax.all_gather(weight, 'fsdp', axis=0, tiled=True)]
    reduce_scatter x5, waiting for transfers between devices: 444 us -> 191 us  [weight_grad(): lax.psum_scatter(term().astype(jnp.bfloat16), 'fsdp', scatter_dimension=0...]
    all_gather x1, blocking collectives: 31.2 us -> 5.16 us  [on_device(): order_all = lax.all_gather(places, 'seq', axis=0, tiled=True)]
    concatenate x0 -> x15, other arithmetic: none -> 25.3 us  [_place_samples(): jnp.concatenate([jnp.where(u_next, big, t1), jnp.where(u_next, t1, big)])]
    dot_general x40, matrix products: 74.3 us -> 97 us  [contract_cols(): lax.dot_general(left, right, (((1,), (1,)), ((), ())), preferred_element_...]
  transfers between devices with their start and end apart: 16 -> 30, of which waited for: 12 -> 17; matrix products, arithmetic and copies ran while one was open for 28% -> 28% of each run, Pallas kernels for 0% -> 0%
where the time goes in v1:
time: 2000 us; the launch traced here: 1980 us
  waiting for transfers between devices  1270 us (64%)
  matrix products  248 us (12%)
  local copies, waits for them, and re-layouts  246 us (12%)
  other arithmetic  103 us (5%)
  blocking collectives  44.8 us (2%)
  loops' own time  30 us (2%)
  starting transfers between devices  29.6 us (1%)
    ppermute x15, waiting for transfers between devices, _place_samples(): lax.ppermute(big, net_axis, [(dd, dd ^ reached) for dd in range(block_now)])  948 us
    reduce_scatter x5, waiting for transfers between devices, weight_grad(): lax.psum_scatter(term().astype(jnp.bfloat16), 'fsdp', scatter_dimension=0...  191 us
    dot_general x40, matrix products, contract_cols(): lax.dot_general(left, right, (((1,), (1,)), ((), ())), preferred_element_...  97 us
    dot_general x28, matrix products, contract_rows(): lax.dot_general(left, right, (((0,), (0,)), ((), ())), preferred_element_...  86.2 us
    psum x1, waiting for transfers between devices, weight_grad(): shard = lax.psum(shard.astype(jnp.bfloat16), 'seq').astype(jnp.float32)  67.7 us
    dynamic_update_slice x24, local copies, waits for them, and re-layouts, head_backward(): lax.scan(step, (zeros, zeros), jnp.arange(group // block))  53.2 us
  transfers between devices with their start and end apart: 30, of which 17 were waited for; matrix products, arithmetic and copies ran while one was open for 28% of the time, Pallas kernels for 0%

profile of v1, /device:TPU:0, one launch (start us, length us, event | category | flops | bytes accessed | tf_op | source)
XLA Modules:
  0.0 1983.1 jit_solution(4169073583891785016)
XLA Ops:
  17.7 5.2 all-gather
  23.6 37.5 %collective-permute-done = bf16[1,32,2048]{2,1,0:T(8,128)(2,1)S(1)} collective-permute-done((bf16[1,32,2048]{2,1,0:T(8,128)(2,1)S(1)}, bf16[1,32,2048]{2,1,0:T(8,128)(2,1)S(1)}, u32[]{:S(2)}, u32[]{:S(2)}) %collective-permute-start) | collective-permute-done | bytes 131104 | tf_op jit(solution)/shard_map/ppermute | solution.py:29
  65.0 6.3 collective-permute-done.6
  73.9 82.9 %collective-permute-done.1 = bf16[2,32,2048]{2,1,0:T(8,128)(2,1)S(1)} collective-permute-done((bf16[2,32,2048]{2,1,0:T(8,128)(2,1)S(1)}, bf16[2,32,2048]{2,1,0:T(8,128)(2,1)S(1)}, u32[]{:S(2)}, u32[]{:S(2)}) %collective-permute-start.1) | collective-permute-done | bytes 262176 | tf_op jit(solution)/shard_map/ppermute | solution.py:29
  157.1 31.6 %collective-permute-done.7 = bf16[2,128,1024]{2,1,0:T(8,128)(2,1)S(1)} collective-permute-done((bf16[2,128,1024]{2,1,0:T(8,128)(2,1)S(1)}, bf16[2,128,1024]{2,1,0:T(8,128)(2,1)S(1)}, u32[]{:S(2)}, u32[]{:S(2)}) %collective-permute-start.7) | collective-permute-done | bytes 524320 | tf_op jit(solution)/shard_map/ppermute | solution.py:29
  192.5 33.4 %collective-permute-done.2 = bf16[4,32,2048]{2,1,0:T(8,128)(2,1)S(1)} collective-permute-done((bf16[4,32,2048]{2,1,0:T(8,128)(2,1)S(1)}, bf16[4,32,2048]{2,1,0:T(8,128)(2,1)S(1)}, u32[]{:S(2)}, u32[]{:S(2)}) %collective-permute-start.2) | collective-permute-done | bytes 524320 | tf_op jit(solution)/shard_map/ppermute | solution.py:29
  237.6 96.0 %collective-permute-done.8 = bf16[4,128,1024]{2,1,0:T(8,128)(2,1)S(1)} collective-permute-done((bf16[4,128,1024]{2,1,0:T(8,128)(2,1)S(1)}, bf16[4,128,1024]{2,1,0:T(8,128)(2,1)S(1)}, u32[]{:S(2)}, u32[]{:S(2)}) %collective-permute-start.8) | collective-permute-done | bytes 1048608 | tf_op jit(solution)/shard_map/ppermute | solution.py:29
  335.2 162.9 %collective-permute-done.5 = bf16[4,128,3072]{2,1,0:T(8,128)(2,1)S(1)} collective-permute-done((bf16[4,128,3072]{2,1,0:T(8,128)(2,1)S(1)}, bf16[4,128,3072]{2,1,0:T(8,128)(2,1)S(1)}, u32[]{:S(2)}, u32[]{:S(2)}) %collective-permute-start.5) | collective-permute-done | bytes 3145760 | tf_op jit(solution)/shard_map/ppermute | solution.py:29
  501.7 4.7 fusion.97
  521.5 4.7 all-to-all-start
  531.3 4.5 fusion.49
  535.8 18.9 all-to-all-done
  559.6 133.9 %while.88 = (s32[]{:T(128)}, bf16[4,1536,64]{1,2,0:T(8,128)(2,1)}, f32[4,1536]{1,0:T(4,128)}, s32[4]{0:T(128)}, bf16[1536,256]{1,0:T(8,128)(2,1)}, /*index=5*/bf...) while((s32[]{:T(128)}, bf16[4,1536,64]{1,2,0:T(8,128)(2,1)}, ...), condition=%wide.region_10.11_spmd, body=%wide.region_5.10_spmd.sunk | while | flops 208436736 | bytes 12641802 | solution.py:228
  565.9 23.0 %while.91 = (s32[]{:T(128)}, bf16[3,512,64]{1,2,0:T(8,128)(2,1)}, f32[3,512]{1,0:T(4,128)}, s32[3]{0:T(128)}, s32[1536]{0:T(1024)S(1)}, /*index=5*/bf16[1536,64]...) while((s32[]{:T(128)}, bf16[3,512,64]{1,2,0:T(8,128)(2,1)}, ...), condition=%wide.region_9.9_spmd, body=%wide.region_6.8_spmd.sunk | while | flops 208436736 | bytes 10257083 | solution.py:156
  599.4 23.0 %while.91 = (s32[]{:T(128)}, bf16[3,512,64]{1,2,0:T(8,128)(2,1)}, f32[3,512]{1,0:T(4,128)}, s32[3]{0:T(128)}, s32[1536]{0:T(1024)S(1)}, /*index=5*/bf16[1536,64]...) while((s32[]{:T(128)}, bf16[3,512,64]{1,2,0:T(8,128)(2,1)}, ...), condition=%wide.region_9.9_spmd, body=%wide.region_6.8_spmd.sunk | while | flops 208436736 | bytes 10257083 | solution.py:156
  632.9 23.0 %while.91 = (s32[]{:T(128)}, bf16[3,512,64]{1,2,0:T(8,128)(2,1)}, f32[3,512]{1,0:T(4,128)}, s32[3]{0:T(128)}, s32[1536]{0:T(1024)S(1)}, /*index=5*/bf16[1536,64]...) while((s32[]{:T(128)}, bf16[3,512,64]{1,2,0:T(8,128)(2,1)}, ...), condition=%wide.region_9.9_spmd, body=%wide.region_6.8_spmd.sunk | while | flops 208436736 | bytes 10257083 | solution.py:156
  666.4 23.0 %while.91 = (s32[]{:T(128)}, bf16[3,512,64]{1,2,0:T(8,128)(2,1)}, f32[3,512]{1,0:T(4,128)}, s32[3]{0:T(128)}, s32[1536]{0:T(1024)S(1)}, /*index=5*/bf16[1536,64]...) while((s32[]{:T(128)}, bf16[3,512,64]{1,2,0:T(8,128)(2,1)}, ...), condition=%wide.region_9.9_spmd, body=%wide.region_6.8_spmd.sunk | while | flops 208436736 | bytes 10257083 | solution.py:156
  699.7 3.7 all-to-all-start.1
  703.4 97.8 %collective-permute-done.11 = bf16[4,128,4096]{2,1,0:T(8,128)(2,1)} collective-permute-done((bf16[4,128,4096]{2,1,0:T(8,128)(2,1)}, bf16[4,128,4096]{2,1,0:T(8,128)(2,1)}, u32[]{:S(2)}, u32[]{:S(2)}) %collective-permute-start.11) | collective-permute-done | bytes 4194336 | tf_op jit(solution)/shard_map/ppermute | solution.py:29
  801.2 5.4 broadcast_select_fusion.3
  806.5 7.5 pad_maximum_fusion
  821.4 8.7 fusion.98
  830.1 12.0 fusion.44
  842.1 8.5 multiply_reduce_fusion.1
  852.7 4.0 convolution_convert_fusion.5
  866.6 8.2 all-to-all-done.2
  875.4 280.9 %while.90 = (s32[]{:T(128)}, bf16[4,1536,64]{1,2,0:T(8,128)(2,1)}, bf16[4,1536,64]{1,2,0:T(8,128)(2,1)}, bf16[4,1536,64]{1,2,0:T(8,128)(2,1)}, s32[4]{0:T(128)},...) while((s32[]{:T(128)}, bf16[4,1536,64]{1,2,0:T(8,128)(2,1)}, ...), condition=%wide.region_20.21_spmd, body=%wide.region_16.20_spmd.sunk | while | flops 513375776 | bytes 51172928 | solution.py:270
  886.7 52.4 %while.92 = (s32[]{:T(128)}, f32[1536,64]{0,1:T(8,128)}, f32[1536,64]{0,1:T(8,128)}, f32[3,512,64]{1,0,2:T(4,128)}, s32[3]{0:T(128)}, /*index=5*/s32[1536]{0:T(1...) while((s32[]{:T(128)}, f32[1536,64]{0,1:T(8,128)}, ...), condition=%wide.region_19.19_spmd.clone, body=%wide.region_17.18_spmd.clone.sunk | while | flops 511704576 | bytes 33446152 | solution.py:183
  956.9 52.3 %while.92 = (s32[]{:T(128)}, f32[1536,64]{0,1:T(8,128)}, f32[1536,64]{0,1:T(8,128)}, f32[3,512,64]{1,0,2:T(4,128)}, s32[3]{0:T(128)}, /*index=5*/s32[1536]{0:T(1...) while((s32[]{:T(128)}, f32[1536,64]{0,1:T(8,128)}, ...), condition=%wide.region_19.19_spmd.clone, body=%wide.region_17.18_spmd.clone.sunk | while | flops 511704576 | bytes 33446152 | solution.py:183
  1027.1 52.3 %while.92 = (s32[]{:T(128)}, f32[1536,64]{0,1:T(8,128)}, f32[1536,64]{0,1:T(8,128)}, f32[3,512,64]{1,0,2:T(4,128)}, s32[3]{0:T(128)}, /*index=5*/s32[1536]{0:T(1...) while((s32[]{:T(128)}, f32[1536,64]{0,1:T(8,128)}, ...), condition=%wide.region_19.19_spmd.clone, body=%wide.region_17.18_spmd.clone.sunk | while | flops 511704576 | bytes 33446152 | solution.py:183
  1097.3 52.3 %while.92 = (s32[]{:T(128)}, f32[1536,64]{0,1:T(8,128)}, f32[1536,64]{0,1:T(8,128)}, f32[3,512,64]{1,0,2:T(4,128)}, s32[3]{0:T(128)}, /*index=5*/s32[1536]{0:T(1...) while((s32[]{:T(128)}, f32[1536,64]{0,1:T(8,128)}, ...), condition=%wide.region_19.19_spmd.clone, body=%wide.region_17.18_spmd.clone.sunk | while | flops 511704576 | bytes 33446152 | solution.py:183
  1159.7 4.3 copy.79
  1163.9 39.6 %all_to_all.63 = bf16[1536,3,1,256]{3,1,2,0:T(4,128)(2,1)S(1)} all-to-all(bf16[1536,3,1,256]{3,1,2,0:T(4,128)(2,1)S(1)} %copy.79), channel_id=1, replica_groups=mesh['seq'=4,'fsdp'=8] {'seq'}, dimensions={0} | all-to-all | bytes 4718592 | tf_op jit(solution)/shard_map/all_to_all | solution.py:125
  1205.3 4.4 copy.81
  1209.8 6.7 fusion.63
  1221.7 10.6 convolution_convert_fusion
  1234.1 5.4 convolution_convert_fusion.2
  1240.7 8.9 convolution_convert_fusion.1
  1252.3 26.2 %collective-permute-done.12 = bf16[1,512,1024]{2,1,0:T(8,128)(2,1)S(1)} collective-permute-done((bf16[1,512,1024]{2,1,0:T(8,128)(2,1)S(1)}, bf16[1,512,1024]{2,1,0:T(8,128)(2,1)S(1)}, u32[]{:S(2)}, u32[]{:S(2)}) %collective-permute-start.12) | collective-permute-done | bytes 1048608 | tf_op jit(solution)/shard_map/ppermute | solution.py:29
  1278.9 106.3 %collective-permute-done.13 = bf16[2,512,1024]{2,1,0:T(8,128)(2,1)S(1)} collective-permute-done((bf16[2,512,1024]{2,1,0:T(8,128)(2,1)S(1)}, bf16[2,512,1024]{2,1,0:T(8,128)(2,1)S(1)}, u32[]{:S(2)}, u32[]{:S(2)}) %collective-permute-start.13) | collective-permute-done | bytes 2097184 | tf_op jit(solution)/shard_map/ppermute | solution.py:29
  1385.9 266.9 %collective-permute-done.14 = bf16[4,512,1024]{2,1,0:T(8,128)(2,1)S(1)} collective-permute-done((bf16[4,512,1024]{2,1,0:T(8,128)(2,1)S(1)}, bf16[4,512,1024]{2,1,0:T(8,128)(2,1)S(1)}, u32[]{:S(2)}, u32[]{:S(2)}) %collective-permute-start.14) | collective-permute-done | bytes 4194336 | tf_op jit(solution)/shard_map/ppermute | solution.py:29
  1656.5 7.7 pad_maximum_fusion.1
  1664.2 10.3 add_convert_fusion
  1674.7 40.6 %reduce-scatter.8.cloned.1.call-done = bf16[128,3072]{1,0:T(8,128)(2,1)} async-done(((bf16[1024,3072]{1,0:T(8,128)(2,1)}), bf16[128,3072]{1,0:T(8,128)(2,1)}) %reduce-scatter.8.cloned.1.call-update) | async-done | bytes 786448 | tf_op jit(solution)/shard_map/reduce_scatter | solution.py:113
  1715.3 150.2 %reduce-scatter.12.cloned.1.call-done = bf16[128,4096]{1,0:T(8,128)(2,1)} async-done(((bf16[1024,4096]{1,0:T(8,128)(2,1)}), bf16[128,4096]{1,0:T(8,128)(2,1)}) %reduce-scatter.12.cloned.1.call-update) | async-done | bytes 1048592 | tf_op jit(solution)/shard_map/reduce_scatter | solution.py:113
  1865.5 29.7 %all-gather.9.cloned.1.call-done = bf16[1536,1024]{1,0:T(8,128)(2,1)} async-done(((bf16[384,1024]{1,0:T(8,128)(2,1)}), bf16[1536,1024]{1,0:T(8,128)(2,1)}) %all-gather.9.cloned.1.call-update) | async-done | bytes 3145744 | tf_op jit(solution)/shard_map/all_gather | solution.py:131
  1895.2 4.2 fusion.69
  1900.8 67.7 %all-reduce.3.cloned.1.call-done = (bf16[32,2048]{1,0:T(8,128)(2,1)}, bf16[128,3072]{1,0:T(8,128)(2,1)}, bf16[128,1024]{1,0:T(8,128)(2,1)}, bf16[128,4096]{1,0:T(8,128)(2,1)}, bf16[512,1024]{1,0:T(8,128)(2,1)}) async-done(((bf16[32,2048]{1,0:T(8,128)(2,1)}, bf16[128,3072]{1,0:T(8,128)(2,1)}, bf16[128,1024]{1,0:T(8,128)(2,1)}, bf16[128,4096]{1,0:T(8,128)(2,1)}, bf16[512,1024]{1,0:T(8,128)(2,1)}), ...) | async-done | bytes 3276816 | tf_op jit(solution)/shard_map/psum | solution.py:116
  (642 shorter events, 503.5 us)
Async XLA Ops:
  7.2 524.1 %all-gather.19.cloned.1.call-start = ((), (), s32[]{:S(2)}) async-start(), calls=%async_computation.19 | async-start | bytes 3932160 | tf_op jit(solution)/shard_map/all_gather | solution.py:131
  8.0 822.1 %all-gather.11.cloned.1.call-start = ((), (), s32[]{:S(2)}) async-start(), calls=%async_computation.10 | async-start | bytes 9437184 | tf_op jit(solution)/shard_map/all_gather | solution.py:97
  8.7 833.4 %all-gather.13.cloned.1.call-start = ((), (), s32[]{:S(2)}) async-start(), calls=%async_computation.11 | async-start | bytes 9437184 | tf_op jit(solution)/shard_map/all_gather | solution.py:97
  9.4 843.3 %all-gather.15.cloned.1.call-start = ((), (), s32[]{:S(2)}) async-start(), calls=%async_computation.12 | async-start | bytes 2359296 | tf_op jit(solution)/shard_map/all_gather | solution.py:97
  10.0 1199.8 %all-gather.17.cloned.1.call-start = ((), (), s32[]{:S(2)}) async-start(), calls=%async_computation.13 | async-start | bytes 7077888 | tf_op jit(solution)/shard_map/all_gather | solution.py:97
  10.1 220.8 %collective-permute-start.9 = (bf16[1,128,4096]{2,1,0:T(8,128)(2,1)}, bf16[1,128,4096]{2,1,0:T(8,128)(2,1)}, u32[]{:S(2)}, u32[]{:S(2)}) collective-permute-start(bf16[1,128,4096]{2,1,0:T(8,128)(2,1)} %bitcast.39), channel_id=1, source_target_pairs={{0,1},{1,0},{2,3},{3,2},{4,5},{5,4},{6,7},{7,6},{8,9},{9,8},{10,11... | collective-permute-start | bytes 3145736 | tf_op jit(solution)/shard_map/ppermute | solution.py:29
  13.1 48.0 %collective-permute-start.3 = (bf16[1,128,3072]{2,1,0:T(8,128)(2,1)S(1)}, bf16[1,128,3072]{2,1,0:T(8,128)(2,1)}, u32[]{:S(2)}, u32[]{:S(2)}) collective-permute-start(bf16[1,128,3072]{2,1,0:T(8,128)(2,1)S(1)} %bitcast.226), channel_id=1, source_target_pairs={{0,1},{1,0},{2,3},{3,2},{4,5},{5,4},{6,7},{7,6},{8,9},{9,8},{10,11... | collective-permute-start | bytes 2359304 | tf_op jit(solution)/shard_map/ppermute | solution.py:29
  13.2 47.9 %collective-permute-start = (bf16[1,32,2048]{2,1,0:T(8,128)(2,1)S(1)}, bf16[1,32,2048]{2,1,0:T(8,128)(2,1)S(1)}, u32[]{:S(2)}, u32[]{:S(2)}) collective-permute-start(bf16[1,32,2048]{2,1,0:T(8,128)(2,1)S(1)} %bitcast.235), channel_id=1, source_target_pairs={{0,1},{1,0},{2,3},{3,2},{4,5},{5,4},{6,7},{7,6},{8,9},{9,8},{10,11... | collective-permute-start | bytes 393224 | tf_op jit(solution)/shard_map/ppermute | solution.py:29
  15.1 56.1 %collective-permute-start.6 = (bf16[1,128,1024]{2,1,0:T(8,128)(2,1)}, bf16[1,128,1024]{2,1,0:T(8,128)(2,1)}, u32[]{:S(2)}, u32[]{:S(2)}) collective-permute-start(bf16[1,128,1024]{2,1,0:T(8,128)(2,1)} %bitcast.37), channel_id=1, source_target_pairs={{0,1},{1,0},{2,3},{3,2},{4,5},{5,4},{6,7},{7,6},{8,9},{9,8},{10,11... | collective-permute-start | bytes 786440 | tf_op jit(solution)/shard_map/ppermute | solution.py:29
  15.3 516.0 %copy-start.38 = (s32[384]{0:T(512)}, s32[384]{0:T(512)S(1)}, u32[]{:S(2)}) copy-start(s32[384]{0:T(512)S(1)} %reduce.4) | copy-start | bytes 4612
  15.5 47.1 %copy-start.51 = (s32[3,1]{0,1:T(1,128)}, s32[3,1]{0,1:T(1,128)S(1)}, u32[]{:S(2)}) copy-start(s32[3,1]{0,1:T(1,128)S(1)} %reduce-window.4) | copy-start | bytes 40
  15.5 47.1 %copy-start.54 = (s32[3]{0:T(128)}, s32[3]{0:T(128)S(1)}, u32[]{:S(2)}) copy-start(s32[3]{0:T(128)S(1)} %fusion.87) | copy-start | bytes 40
  15.7 212.1 %copy-start.41 = (f32[384]{0:T(512)}, f32[384]{0:T(512)S(1)}, u32[]{:S(2)}) copy-start(f32[384]{0:T(512)S(1)} %broadcast_multiply_fusion.1) | copy-start | bytes 4612
  22.9 39.9 %copy-start.35 = (s32[1536]{0:T(1024)}, s32[1536]{0:T(1024)S(1)}, u32[]{:S(2)}) copy-start(s32[1536]{0:T(1024)S(1)} %reduce.3) | copy-start | bytes 18436
  62.8 126.2 %collective-permute-start.4 = (bf16[2,128,3072]{2,1,0:T(8,128)(2,1)S(1)}, bf16[2,128,3072]{2,1,0:T(8,128)(2,1)S(1)}, u32[]{:S(2)}, u32[]{:S(2)}) collective-permute-start(bf16[2,128,3072]{2,1,0:T(8,128)(2,1)S(1)} %pad_maximum_fusion.11), channel_id=1, source_target_pairs={{0,2},{1,3},{2,0},{3,1},{4,6},{5,7},{6,4},{7,5},{8,10},{9,11},{10,... | collective-permute-start | bytes 4718600 | tf_op jit(solution)/shard_map/ppermute | solution.py:29
  64.3 92.6 %collective-permute-start.1 = (bf16[2,32,2048]{2,1,0:T(8,128)(2,1)S(1)}, bf16[2,32,2048]{2,1,0:T(8,128)(2,1)S(1)}, u32[]{:S(2)}, u32[]{:S(2)}) collective-permute-start(bf16[2,32,2048]{2,1,0:T(8,128)(2,1)S(1)} %pad_maximum_fusion.18), channel_id=1, source_target_pairs={{0,2},{1,3},{2,0},{3,1},{4,6},{5,7},{6,4},{7,5},{8,10},{9,11},{10,... | collective-permute-start | bytes 786440 | tf_op jit(solution)/shard_map/ppermute | solution.py:29
  72.4 116.3 %collective-permute-start.7 = (bf16[2,128,1024]{2,1,0:T(8,128)(2,1)S(1)}, bf16[2,128,1024]{2,1,0:T(8,128)(2,1)S(1)}, u32[]{:S(2)}, u32[]{:S(2)}) collective-permute-start(bf16[2,128,1024]{2,1,0:T(8,128)(2,1)S(1)} %pad_maximum_fusion.17), channel_id=1, source_target_pairs={{0,2},{1,3},{2,0},{3,1},{4,6},{5,7},{6,4},{7,5},{8,10},{9,11},{10,... | collective-permute-start | bytes 1572872 | tf_op jit(solution)/shard_map/ppermute | solution.py:29
  157.0 68.9 %collective-permute-start.2 = (bf16[4,32,2048]{2,1,0:T(8,128)(2,1)S(1)}, bf16[4,32,2048]{2,1,0:T(8,128)(2,1)S(1)}, u32[]{:S(2)}, u32[]{:S(2)}) collective-permute-start(bf16[4,32,2048]{2,1,0:T(8,128)(2,1)S(1)} %pad_maximum_fusion.16), channel_id=1, source_target_pairs={{0,4},{1,5},{2,6},{3,7},{4,0},{5,1},{6,2},{7,3},{8,12},{9,13},{10,... | collective-permute-start | bytes 1572872 | tf_op jit(solution)/shard_map/ppermute | solution.py:29
  188.9 144.7 %collective-permute-start.8 = (bf16[4,128,1024]{2,1,0:T(8,128)(2,1)S(1)}, bf16[4,128,1024]{2,1,0:T(8,128)(2,1)S(1)}, u32[]{:S(2)}, u32[]{:S(2)}) collective-permute-start(bf16[4,128,1024]{2,1,0:T(8,128)(2,1)S(1)} %pad_maximum_fusion.13), channel_id=1, source_target_pairs={{0,4},{1,5},{2,6},{3,7},{4,0},{5,1},{6,2},{7,3},{8,12},{9,13},{10,... | collective-permute-start | bytes 3145736 | tf_op jit(solution)/shard_map/ppermute | solution.py:29
  189.5 36.6 %copy-start.47 = (bf16[3,128]{1,0:T(4,128)(2,1)S(1)}, bf16[3,128]{1,0:T(4,128)(2,1)}, u32[]{:S(2)}) copy-start(bf16[3,128]{1,0:T(4,128)(2,1)} %get-tuple-element.581) | copy-start | bytes 2308
  189.5 36.6 %copy-start.49 = (bf16[3,128]{1,0:T(4,128)(2,1)S(1)}, bf16[3,128]{1,0:T(4,128)(2,1)}, u32[]{:S(2)}) copy-start(bf16[3,128]{1,0:T(4,128)(2,1)} %get-tuple-element.582) | copy-start | bytes 2308
  189.5 36.8 %copy-start.52 = (s32[3,1]{0,1:T(1,128)S(1)}, s32[3,1]{0,1:T(1,128)}, u32[]{:S(2)}) copy-start(s32[3,1]{0,1:T(1,128)} %copy-done.51) | copy-start | bytes 40
  189.5 36.8 %copy-start.55 = (s32[3]{0:T(128)S(1)}, s32[3]{0:T(128)}, u32[]{:S(2)}) copy-start(s32[3]{0:T(128)} %copy-done.54) | copy-start | bytes 40
  189.5 308.6 %collective-permute-start.5 = (bf16[4,128,3072]{2,1,0:T(8,128)(2,1)S(1)}, bf16[4,128,3072]{2,1,0:T(8,128)(2,1)S(1)}, u32[]{:S(2)}, u32[]{:S(2)}) collective-permute-start(bf16[4,128,3072]{2,1,0:T(8,128)(2,1)S(1)} %pad_maximum_fusion.5), channel_id=1, source_target_pairs={{0,4},{1,5},{2,6},{3,7},{4,0},{5,1},{6,2},{7,3},{8,12},{9,13},{10,... | collective-permute-start | bytes 9437192 | tf_op jit(solution)/shard_map/ppermute | solution.py:29
  234.0 292.1 %collective-permute-start.10 = (bf16[2,128,4096]{2,1,0:T(8,128)(2,1)}, bf16[2,128,4096]{2,1,0:T(8,128)(2,1)}, u32[]{:S(2)}, u32[]{:S(2)}) collective-permute-start(bf16[2,128,4096]{2,1,0:T(8,128)(2,1)} %pad_maximum_fusion.9), channel_id=1, source_target_pairs={{0,2},{1,3},{2,0},{3,1},{4,6},{5,7},{6,4},{7,5},{8,10},{9,11},{10,... | collective-permute-start | bytes 6291464 | tf_op jit(solution)/shard_map/ppermute | solution.py:29
  521.5 33.2 %all-to-all-start = ((bf16[384,3,4,256]{0,3,1,2:T(8,128)(2,1)}), bf16[384,3,4,256]{0,3,1,2:T(8,128)(2,1)}, u32[]{:S(2)}, u32[]{:S(2)}) async-start(bf16[384,3,4,256]{0,3,1,2:T(8,128)(2,1)} %copy.73), calls=%async_computation | async-start | bytes 4718592 | tf_op jit(solution)/shard_map/all_to_all | solution.py:121
  531.3 269.8 %collective-permute-start.11 = (bf16[4,128,4096]{2,1,0:T(8,128)(2,1)}, bf16[4,128,4096]{2,1,0:T(8,128)(2,1)}, u32[]{:S(2)}, u32[]{:S(2)}) collective-permute-start(bf16[4,128,4096]{2,1,0:T(8,128)(2,1)} %pad_maximum_fusion.3), channel_id=1, source_target_pairs={{0,4},{1,5},{2,6},{3,7},{4,0},{5,1},{6,2},{7,3},{8,12},{9,13},{10,... | collective-permute-start | bytes 12582920 | tf_op jit(solution)/shard_map/ppermute | solution.py:29
  696.5 104.6 %copy-start.10 = (bf16[2,128,4096]{2,1,0:T(8,128)(2,1)S(1)}, bf16[2,128,4096]{2,1,0:T(8,128)(2,1)}, u32[]{:S(2)}) copy-start(bf16[2,128,4096]{2,1,0:T(8,128)(2,1)} %copy-done.9) | copy-start | bytes 6291460
  699.7 114.4 %all-to-all-start.1 = ((bf16[4,2,49152]{2,1,0:T(2,128)(2,1)}), bf16[4,2,49152]{2,1,0:T(2,128)(2,1)S(1)}, u32[]{:S(2)}, u32[]{:S(2)}) async-start(bf16[4,2,49152]{2,1,0:T(2,128)(2,1)} %reshape.403), calls=%async_computation.1 | async-start | bytes 1572864 | tf_op jit(solution)/shard_map/all_to_all | solution.py:125
  852.7 11.3 copy-start.12
  859.8 15.1 all-to-all-start.2
  863.3 811.4 %reduce-scatter.10.cloned.1.call-start = ((), (), s32[]{:S(2)}) async-start(), calls=%async_computation.16 | async-start | bytes 2359296 | tf_op jit(solution)/shard_map/reduce_scatter | solution.py:113
  866.6 808.1 %reduce-scatter.6.cloned.1.call-start = ((), (), s32[]{:S(2)}) async-start(), calls=%async_computation.14 | async-start | bytes 1179648 | tf_op jit(solution)/shard_map/reduce_scatter | solution.py:113
  875.6 11.1 copy-start.14
  945.9 11.1 copy-start.14
  1016.0 11.1 copy-start.14
  1086.2 11.1 copy-start.14
  1221.6 453.1 %reduce-scatter.14.cloned.1.call-start = ((), (), s32[]{:S(2)}) async-start(), calls=%async_computation.18 | async-start | bytes 9437184 | tf_op jit(solution)/shard_map/reduce_scatter | solution.py:113
  1232.3 483.0 %reduce-scatter.8.cloned.1.call-start = ((), (), s32[]{:S(2)}) async-start(), calls=%async_computation.15 | async-start | bytes 7077888 | tf_op jit(solution)/shard_map/reduce_scatter | solution.py:113
  1239.5 625.9 %reduce-scatter.12.cloned.1.call-start = ((), (), s32[]{:S(2)}) async-start(), calls=%async_computation.17 | async-start | bytes 9437184 | tf_op jit(solution)/shard_map/reduce_scatter | solution.py:113
  1249.5 645.7 %all-gather.9.cloned.1.call-start = ((), (), s32[]{:S(2)}) async-start(), calls=%async_computation.9 | async-start | bytes 3932160 | tf_op jit(solution)/shard_map/all_gather | solution.py:131
  1250.8 27.7 %collective-permute-start.12 = (bf16[1,512,1024]{2,1,0:T(8,128)(2,1)S(1)}, bf16[1,512,1024]{2,1,0:T(8,128)(2,1)S(1)}, u32[]{:S(2)}, u32[]{:S(2)}) collective-permute-start(bf16[1,512,1024]{2,1,0:T(8,128)(2,1)S(1)} %bitcast.220), channel_id=1, source_target_pairs={{0,1},{1,0},{2,3},{3,2},{4,5},{5,4},{6,7},{7,6},{8,9},{9,8},{10,11... | collective-permute-start | bytes 3145736 | tf_op jit(solution)/shard_map/ppermute | solution.py:29
  1278.8 106.4 %collective-permute-start.13 = (bf16[2,512,1024]{2,1,0:T(8,128)(2,1)S(1)}, bf16[2,512,1024]{2,1,0:T(8,128)(2,1)S(1)}, u32[]{:S(2)}, u32[]{:S(2)}) collective-permute-start(bf16[2,512,1024]{2,1,0:T(8,128)(2,1)S(1)} %pad_maximum_fusion.10), channel_id=1, source_target_pairs={{0,2},{1,3},{2,0},{3,1},{4,6},{5,7},{6,4},{7,5},{8,10},{9,11},{10,... | collective-permute-start | bytes 6291464 | tf_op jit(solution)/shard_map/ppermute | solution.py:29
  1385.8 267.0 %collective-permute-start.14 = (bf16[4,512,1024]{2,1,0:T(8,128)(2,1)S(1)}, bf16[4,512,1024]{2,1,0:T(8,128)(2,1)S(1)}, u32[]{:S(2)}, u32[]{:S(2)}) collective-permute-start(bf16[4,512,1024]{2,1,0:T(8,128)(2,1)S(1)} %pad_maximum_fusion.4), channel_id=1, source_target_pairs={{0,4},{1,5},{2,6},{3,7},{4,0},{5,1},{6,2},{7,3},{8,12},{9,13},{10,... | collective-permute-start | bytes 12582920 | tf_op jit(solution)/shard_map/ppermute | solution.py:29
  1674.5 220.7 %copy-start.37 = (s32[1536]{0:T(1024)S(1)}, s32[1536]{0:T(1024)}, u32[]{:S(2)}) copy-start(s32[1536]{0:T(1024)} %copy-done.35) | copy-start | bytes 18436
  1674.6 293.9 %all-reduce.3.cloned.1.call-start = ((), (), s32[]{:S(2)}) async-start(), calls=%async_computation.20 | async-start | bytes 6553600 | tf_op jit(solution)/shard_map/psum | solution.py:116
  1865.5 34.0 %copy-start.13 = (f32[384,1024]{1,0:T(8,128)S(1)}, f32[384,1024]{1,0:T(8,128)}, u32[]{:S(2)}) copy-start(f32[384,1024]{1,0:T(8,128)} %copy-done.12) | copy-start | bytes 4718596
  1865.5 34.0 %copy-start.18 = (f32[384,1024]{1,0:T(8,128)S(1)}, f32[384,1024]{1,0:T(8,128)}, u32[]{:S(2)}) copy-start(f32[384,1024]{1,0:T(8,128)} %get-tuple-element.519) | copy-start | bytes 4718596
  (65 other events, 232.1 us)
Sparse Core Ops, SparseCore 0:
  9.6 31.2 all-gather.18
  43.0 271.2 all-gather.10
  316.5 180.1 all-gather.12
  498.7 141.0 all-gather.14
  641.8 133.0 all-gather.16
  867.9 67.6 reduce-scatter.9
  1221.7 63.4 reduce-scatter.5
  1288.8 282.6 reduce-scatter.13
  1575.1 140.1 reduce-scatter.7
  1718.7 146.6 reduce-scatter.11
  1867.6 27.6 all-gather.8
  1897.8 70.6 all-reduce.2
